TPU v7x, 256 devices: a 4x2x16 block of a 4x16x16 slice. The times are simulated.
256 devices in a mesh: rep: 2 (over y), step: 32 (over z, core), patch: 4 (over x).
Axes of the slice: x: 4, y: 2, z: 16, core: 2. Of those that a mesh axis runs over, the one named last changes fastest.
The devices are a block of a 4x16x16 slice.
Arguments:
- latent_old: float32 [64, 1024, 64], P(('rep', 'step'), 'patch'), parts along dimension 0, may hold values from -6 to 6
- noise_start: float32 [2048, 64], P(('rep', 'patch')), parts along dimension 0, may hold values from -6 to 6
- step_index: int32 [64], P(('rep', 'step')), parts along dimension 0, may hold values from 0 to 998
- sigma_table: float32 [1000], replicated, may hold values from 0.02 to 1
- mod_weight: bfloat16 [256, 9216], replicated, may hold values from -0.375 to 0.375
- embed_weight: bfloat16 [64, 3072], replicated, may hold values from -0.75 to 0.75
- embed_bias: float32 [3072], replicated, may hold values from -3 to 3
- query_weight: bfloat16 [3072, 1536], P('step'), may hold values from -0.109375 to 0.109375
- query_gain: float32 [128], replicated, may hold values from 0.1 to 1.9
- stale_keys: bfloat16 [64, 1280, 1536], P(('rep', 'step'), 'patch'), parts along dimension 0, may hold values from -640 to 640
- stale_values: bfloat16 [64, 1280, 1536], P(('rep', 'step'), 'patch'), parts along dimension 0, may hold values from -6 to 6
- out_weight: bfloat16 [3072, 1536], P('step'), may hold values from -0.3125 to 0.3125
- final_weight: bfloat16 [3072, 64], replicated, may hold values from -0.109375 to 0.109375
Outputs:
- latent_new: float32 [64, 1024, 64], P(('rep', 'step'), 'patch'), parts along dimension 0
There are 2 independent parts, one for each index of `rep`. A program takes and returns all parts, laid end to end along the dimension named above; an argument that names none is the same for every part. Nothing has to cross between parts.
All inputs are finite; a program needn't handle non-finite values.
Results may differ from a plain program's by a relative error of at most 0.012.
The roundings to bfloat16 on the way count: a program that leaves them out, or rounds other values in their place, can miss the bound.
Values may be sent and summed in bfloat16 or wider, within the bound.
No kernel may reach another device: no remote copies, remote signals or barrier semaphores. Data moves between devices by JAX's collectives and lax.ppermute only.
A program may use at most 128 MiB of HBM per device.

v0:
```python
import math
import jax
import jax.numpy as jnp
from jax import lax
from jax.sharding import Mesh
from jax.sharding import PartitionSpec as P

D = 3072
HEAD = 128
FREQ = 256
STEP = ("step_0", "step_1")
REP_STEP = ("rep", "step_0", "step_1")
epsilon = 1e-06


def from_everyone(shard, axis):
    copies = jnp.broadcast_to(shard, (lax.axis_size(axis), *shard.shape))
    return lax.all_to_all(copies, axis, split_axis=0, concat_axis=0, tiled=True)


def in_order(pieces, dim):
    dims = list(pieces.shape[1:])
    dims[dim] *= pieces.shape[0]
    return jnp.moveaxis(pieces, 0, dim).reshape(dims)


def gather_directly(shard, axis, dim):
    pieces = from_everyone(shard, axis)
    return in_order(pieces, dim)


def side_by_side(arrays, axis, dim, along):
    ends, at = ([], 0)
    for a in arrays[:-1]:
        at += a.shape[along]
        ends.append(at)
    both = jnp.concatenate(arrays, axis=along)
    return tuple(jnp.split(gather_directly(both, axis, dim), ends, axis=along))


def neutral_like(shard, identity):
    return jnp.zeros_like(shard) + jnp.asarray(identity, shard.dtype)


def entering(shard, axes, combine, identity):
    before = start = neutral_like(shard, identity)
    running = shard
    for axis in reversed(axes):
        devices, here = (lax.axis_size(axis), lax.axis_index(axis))
        pieces = lax.all_gather(running.astype(jnp.bfloat16), axis)
        inside, running = (start, start)
        for k in range(devices):
            passed = k < here
            running = combine(running, pieces[k].astype(shard.dtype))
            inside = jnp.where(passed, running, inside)
        before = combine(inside, before)
    return before


def layer_norm(values_in):
    row_mean = jnp.mean(values_in, axis=-1, keepdims=True)
    centered = values_in - row_mean
    row_var = jnp.mean(centered * centered, axis=-1, keepdims=True)
    return centered * lax.rsqrt(row_var + epsilon)


def time_embed(sigma_now):
    half_count = FREQ // 2
    frequency = jnp.exp(
        -math.log(10000.0) * jnp.arange(half_count).astype(jnp.float32) / half_count
    )
    angles = 1000.0 * sigma_now * frequency
    return jnp.concatenate([jnp.cos(angles), jnp.sin(angles)])


def project_back(attended, weight_rows):
    return lax.dot_general(
        attended, weight_rows, (((1,), (1,)), ((), ())), preferred_element_type=jnp.float32
    )


def norm_queries(raw_queries, query_gain):
    token_count = raw_queries.shape[0]
    head_count = raw_queries.shape[1] // HEAD
    queries = raw_queries.reshape(token_count, head_count, HEAD)
    queries = (
        queries
        * lax.rsqrt(jnp.mean(queries * queries, axis=-1, keepdims=True) + epsilon)
        * query_gain
    )
    return queries.astype(jnp.bfloat16)


def empty_state(queries):
    token_count = queries.shape[0]
    head_count = queries.shape[1]
    return (
        jnp.full((head_count, token_count), -jnp.inf, jnp.float32),
        jnp.zeros((head_count, token_count), jnp.float32),
        jnp.zeros((head_count, token_count, HEAD), jnp.float32),
    )


def attend_block(queries, state_tuple, key_piece, value_piece):
    head_count = queries.shape[1]
    row_count = key_piece.shape[0]
    key_split = key_piece.reshape(row_count, head_count, HEAD)
    value_split = value_piece.reshape(row_count, head_count, HEAD)
    run_peak, run_total, run_sum = state_tuple
    scores = jnp.einsum(
        "qhd,khd->hqk", queries, key_split, preferred_element_type=jnp.float32
    ) / math.sqrt(HEAD)
    new_peak = jnp.max(scores, axis=-1)
    rescale = jnp.exp(run_peak - new_peak)
    exp_weights = jnp.exp(scores - new_peak[..., None])
    run_total = run_total * rescale + jnp.sum(exp_weights, axis=-1)
    run_sum = run_sum * rescale[..., None] + jnp.einsum(
        "hqk,khd->hqd",
        exp_weights.astype(jnp.bfloat16),
        value_split,
        preferred_element_type=jnp.float32,
    )
    return (new_peak, run_total, run_sum)


def finish_heads(state_tuple):
    final_peak, final_total, final_sum = state_tuple
    blended = final_sum / final_total[..., None]
    token_count = blended.shape[1]
    return jnp.transpose(blended, (1, 0, 2)).reshape(token_count, -1).astype(jnp.bfloat16)


def per_device(
    latent_old,
    noise_start,
    step_index,
    sigma_table,
    mod_weight,
    embed_weight,
    embed_bias,
    query_weight,
    query_gain,
    stale_keys,
    stale_values,
    out_weight,
    final_weight,
):
    step_slot = step_index[0]
    table_slots = jnp.arange(sigma_table.shape[0])
    sigma_now = jnp.sum(jnp.where(table_slots == step_slot, sigma_table, 0.0))
    sigma_next = jnp.sum(jnp.where(table_slots == step_slot + 1, sigma_table, 0.0))
    embedded = jax.nn.silu(time_embed(sigma_now)).astype(jnp.bfloat16)
    modulate = jnp.dot(embedded[None, :], mod_weight, preferred_element_type=jnp.float32)[0]
    width = D
    shift_vec = modulate[:width]
    scale_vec = modulate[width : 2 * width]
    gate_vec = modulate[2 * width :]
    latent = latent_old[0]
    token_count = latent.shape[0]
    hidden = (
        jnp.dot(latent.astype(jnp.bfloat16), embed_weight, preferred_element_type=jnp.float32)
        + embed_bias
    )
    normed = (layer_norm(hidden) * (1.0 + scale_vec) + shift_vec).astype(jnp.bfloat16)
    raw_queries = jnp.dot(
        normed,
        lax.all_gather(query_weight, STEP, axis=0, tiled=True),
        preferred_element_type=jnp.float32,
    )
    queries = norm_queries(raw_queries, query_gain)
    pieces = side_by_side((stale_keys[0], stale_values[0]), "patch", 0, 1)
    final_state = attend_block(queries, empty_state(queries), pieces[0], pieces[1])
    attended = finish_heads(final_state)
    branch = project_back(attended, lax.all_gather(out_weight, STEP, axis=0, tiled=True))
    mixed = hidden + gate_vec * branch
    velocity = jnp.dot(
        layer_norm(mixed).astype(jnp.bfloat16), final_weight, preferred_element_type=jnp.float32
    )
    drift_term = velocity * (sigma_next - sigma_now)
    flat_term = drift_term.reshape(-1, 128)

    def add_terms(earlier, later):
        return earlier + later

    prefix = entering(flat_term, STEP, add_terms, jnp.zeros_like(flat_term))
    result = noise_start + (prefix + flat_term).reshape(token_count, -1)
    return result[None]


def solution(mesh):
    torus = Mesh(
        mesh.devices.reshape(mesh.shape["rep"], 16, 2, mesh.shape["patch"]),
        ("rep", "step_0", "step_1", "patch"),
    )
    placed = (
        P(REP_STEP, "patch", None),
        P(("rep", "patch"), None),
        P(REP_STEP),
        P(),
        P(),
        P(),
        P(),
        P(STEP, None),
        P(),
        P(REP_STEP, "patch", None),
        P(REP_STEP, "patch", None),
        P(STEP, None),
        P(),
    )
    return jax.shard_map(
        per_device,
        mesh=torus,
        in_specs=placed,
        out_specs=P(REP_STEP, "patch", None),
        check_vma=False,
    )
```

profile of v0, /device:TPU:36, one launch (start us, length us, event | category | flops | bytes accessed | tf_op | source)
XLA Modules:
  0.0 225.6 jit_solution(14928748804721785456)
XLA Ops:
  6.6 0.7 all-gather.3.cloned.1.call-update
  7.4 0.7 all-gather.5.cloned.1.call-update
  8.1 1.7 pad_maximum_fusion
  9.8 4.1 %broadcast_in_dim.17 = bf16[4,320,3072]{2,1,0:T(8,128)(2,1)} broadcast(bf16[320,3072]{1,0:T(8,128)(2,1)S(1)} %pad_maximum_fusion), dimensions={1,2} | broadcast | bytes 9830400 | tf_op jit(solution)/shard_map/broadcast_in_dim | solution.py:17
  13.9 24.9 %all-to-all-start = ((bf16[4,320,3072]{2,1,0:T(8,128)(2,1)}), bf16[4,320,3072]{2,1,0:T(8,128)(2,1)}, u32[]{:S(2)}, u32[]{:S(2)}) async-start(bf16[4,320,3072]{2,1,0:T(8,128)(2,1)} %broadcast_in_dim.17), calls=%async_computation | async-start | bytes 15728640 | tf_op jit(solution)/shard_map/all_to_all | solution.py:18
  39.4 0.6 select_reduce_fusion
  42.0 1.5 fusion.46
  43.5 0.5 multiply_reduce_fusion.2
  44.0 3.2 %fusion.49 = f32[1,9216]{1,0:T(1,128)S(1)} fusion(bf16[256,1]{0,1:T(2,128)(2,1)S(1)} %reshape.197, bf16[256,9216]{1,0:T(8,128)(2,1)} %param.17), kind=kOutput, calls=%fused_computation.92 | convolution fusion | flops 4718592 | bytes 4755968 | tf_op jit(solution)/shard_map/dot_general | solution.py:153
  47.2 58.1 %all-to-all-done = bf16[4,320,3072]{2,1,0:T(8,128)(2,1)} async-done(((bf16[4,320,3072]{2,1,0:T(8,128)(2,1)}), bf16[4,320,3072]{2,1,0:T(8,128)(2,1)}, u32[]{:S(2)}, u32[]{:S(2)}) %all-to-all-start) | async-done | bytes 7864352 | tf_op jit(solution)/shard_map/all_to_all | solution.py:18
  105.3 5.5 %fusion.44 = (bf16[1280,1536]{1,0:T(8,128)(2,1)}, bf16[1280,1536]{1,0:T(8,128)(2,1)}) fusion(bf16[1280,3072]{1,0:T(8,128)(2,1)} %bitcast.6), kind=kLoop, calls=%fused_computation.87 | loop fusion | bytes 15728640 | tf_op jit(solution)/shard_map/split | solution.py:38
  110.9 6.3 %copy.31 = bf16[1280,1536]{0,1:T(8,128)(2,1)} copy(bf16[1280,1536]{1,0:T(8,128)(2,1)} %get-tuple-element.8) | data formatting | bytes 7864320 | tf_op jit(solution)/shard_map/split | solution.py:38
  117.2 6.2 %copy.28 = bf16[1280,1536]{0,1:T(8,128)(2,1)} copy(bf16[1280,1536]{1,0:T(8,128)(2,1)} %get-tuple-element.7) | data formatting | bytes 7864320 | tf_op jit(solution)/shard_map/split | solution.py:38
  123.4 6.9 %fusion.7 = f32[256,1536]{0,1:T(8,128)S(1)} fusion(bf16[3072,1536]{1,0:T(8,128)(2,1)} %all-gather.3.cloned.1.call-done, f32[256,3072]{1,0:T(8,128)S(1)} %get-tuple-element.15, f32[3072]{0:T(1024)S(1)} %get-tuple-element.12, f32[3072]{0:T(1024)S(1)} %get-tuple-element.13, f32[256]{0:T(256)S(1)} %add_rsqrt_fusion.2, f32[256]{0:T(256)S(1)} %broadcast_multiply_fusion.1), kind=kOutput, calls=%fused_computation.15 | convolution fusion | flops 2419851264 | bytes 14182400 | tf_op jit(solution)/shard_map/dot_general | solution.py:165
  130.3 0.1 multiply_reduce_fusion.3
  130.5 2.4 %multiply_reduce_fusion = (f32[12,256]{1,0:T(8,128)S(1)}, f32[12,256,1280]{2,1,0:T(8,128)S(1)}) fusion(bf16[1280,12,128]{0,2,1:T(8,128)(2,1)S(1)} %bitcast.39, f32[256,12,128]{0,2,1:T(8,128)S(1)} %bitcast.41, f32[128]{0:T(128)S(1)} %copy-done.8, f32[256,12]{0,1:T(8,128)S(1)} %add_rsqrt_fusion), kind=kOutput, calls=%fused_computation.1 | convolution fusion | flops 1015673856 | bytes 21258752 | tf_op jit(solution)/shard_map/qhd,khd->hqk/dot_general | solution.py:110
  132.9 3.3 %fusion = f32[12,256]{1,0:T(8,128)S(1)} fusion(f32[12,256,1280]{2,1,0:T(8,128)S(1)} %get-tuple-element.17, f32[12,256]{1,0:T(8,128)S(1)} %get-tuple-element.16), kind=kLoop, calls=%fused_computation.2 | loop fusion | flops 11793408 | bytes 15753216 | tf_op jit(solution)/shard_map/reduce_sum | solution.py:116
  136.3 2.2 copy-done.2
  138.5 11.0 %fusion.10 = bf16[256,12,128]{0,2,1:T(8,128)(2,1)} fusion(bf16[1280,12,128]{0,2,1:T(8,128)(2,1)} %bitcast.42, f32[12,256,1280]{2,1,0:T(8,128)} %copy-done.2, f32[12,256]{1,0:T(8,128)S(1)} %get-tuple-element.16, f32[256,12]{0,1:T(8,128)S(1)} %bitcast_add_fusion.1, f32[256,12]{0,1:T(8,128)S(1)} %multiply_bitcast_fusion), kind=kOutput, calls=%fused_computation.19 | convolution fusion | flops 1019609088 | bytes 20484096 | tf_op jit(solution)/shard_map/hqk,khd->hqd/dot_general | solution.py:117
  149.5 27.1 %all-gather.5.cloned.1.call-done = bf16[3072,1536]{1,0:T(8,128)(2,1)} async-done(((bf16[96,1536]{1,0:T(8,128)(2,1)}), bf16[3072,1536]{1,0:T(8,128)(2,1)}) %all-gather.5.cloned.1.call-update) | async-done | bytes 9437200 | tf_op jit(solution)/shard_map/all_gather | solution.py:174
  176.6 5.6 %fusion.47 = (f32[256]{0:T(256)S(1)}, f32[256,3072]{1,0:T(8,128)S(1)}) fusion(f32[256,3072]{1,0:T(8,128)S(1)} %get-tuple-element.15, bf16[256,1536]{0,1:T(8,128)(2,1)} %bitcast.46, bf16[3072,1536]{1,0:T(8,128)(2,1)} %all-gather.5.cloned.1.call-done, f32[3072]{0:T(1024)S(1)} %get-tuple-element.11), kind=kOutput, calls=%fused_computation.90 | convolution fusion | flops 2418278144 | bytes 16528384 | tf_op jit(solution)/shard_map/dot_general | solution.py:77
  182.3 0.5 multiply_reduce_fusion.1
  182.7 0.5 copy-done.4
  183.2 0.7 fusion.48
  183.9 0.1 copy.32
  184.0 0.1 convert_element_type.175
  184.1 1.9 all_gather.16
  186.1 31.1 %all_gather.17 = bf16[16,128,128]{2,1,0:T(8,128)(2,1)S(1)} all-gather(bf16[1,128,128]{2,1,0:T(8,128)(2,1)S(1)} %get-tuple-element.9), channel_id=1, replica_groups=mesh['rep'=2,'step_0'=16,'step_1'=2,'patch'=4] {'step_0'}, dimensions={0}, use_global_device_ids=true | all-gather | bytes 557056 | tf_op jit(solution)/shard_map/all_gather | solution.py:50
  217.3 0.1 select_n.183
  217.4 0.1 reshape.194
  217.6 0.1 fusion.36
  218.1 0.7 add_bitcast_fusion
  (39 shorter events, 0.8 us)
Async XLA Ops:
  6.5 35.4 %copy-start = (bf16[64,3072]{1,0:T(8,128)(2,1)S(1)}, bf16[64,3072]{1,0:T(8,128)(2,1)}, u32[]{:S(2)}) copy-start(bf16[64,3072]{1,0:T(8,128)(2,1)} %param.18) | copy-start | bytes 1179652
  6.6 116.8 %all-gather.3.cloned.1.call-start = ((), (), s32[]{:S(2)}) async-start(), calls=%async_computation.1 | async-start | bytes 9732096 | tf_op jit(solution)/shard_map/all_gather | solution.py:167
  7.3 169.3 %all-gather.5.cloned.1.call-start = ((), (), s32[]{:S(2)}) async-start(), calls=%async_computation.2 | async-start | bytes 9732096 | tf_op jit(solution)/shard_map/all_gather | solution.py:174
  13.9 25.5 %copy-start.7 = (f32[1000]{0:T(1024)S(1)}, f32[1000]{0:T(1024)}, u32[]{:S(2)}) copy-start(f32[1000]{0:T(1024)} %param.16) | copy-start | bytes 12004
  13.9 28.1 %copy-start.6 = (f32[3072]{0:T(1024)S(1)}, f32[3072]{0:T(1024)}, u32[]{:S(2)}) copy-start(f32[3072]{0:T(1024)} %param.19) | copy-start | bytes 36868
  13.9 91.4 %all-to-all-start = ((bf16[4,320,3072]{2,1,0:T(8,128)(2,1)}), bf16[4,320,3072]{2,1,0:T(8,128)(2,1)}, u32[]{:S(2)}, u32[]{:S(2)}) async-start(bf16[4,320,3072]{2,1,0:T(8,128)(2,1)} %broadcast_in_dim.17), calls=%async_computation | async-start | bytes 15728640 | tf_op jit(solution)/shard_map/all_to_all | solution.py:18
  123.4 7.1 %copy-start.3 = (bf16[1280,1536]{0,1:T(8,128)(2,1)S(1)}, bf16[1280,1536]{0,1:T(8,128)(2,1)}, u32[]{:S(2)}) copy-start(bf16[1280,1536]{0,1:T(8,128)(2,1)} %copy.28) | copy-start | bytes 11796484
  123.4 7.1 %copy-start.8 = (f32[128]{0:T(128)S(1)}, f32[128]{0:T(128)}, u32[]{:S(2)}) copy-start(f32[128]{0:T(128)} %param.21) | copy-start | bytes 1540
  132.9 5.5 %copy-start.2 = (f32[12,256,1280]{2,1,0:T(8,128)}, f32[12,256,1280]{2,1,0:T(8,128)S(1)}, u32[]{:S(2)}) copy-start(f32[12,256,1280]{2,1,0:T(8,128)S(1)} %get-tuple-element.17) | copy-start | bytes 47185924
  182.2 1.0 copy-start.4
  182.7 36.0 %copy-start.1 = (bf16[64,3072]{1,0:T(8,128)(2,1)S(1)}, bf16[64,3072]{1,0:T(8,128)(2,1)}, u32[]{:S(2)}) copy-start(bf16[64,3072]{1,0:T(8,128)(2,1)} %param.18) | copy-start | bytes 1179652
  183.2 34.8 %copy-start.5 = (f32[256,64]{0,1:T(8,128)S(1)}, f32[256,64]{0,1:T(8,128)}, u32[]{:S(2)}) copy-start(f32[256,64]{0,1:T(8,128)} %param.14) | copy-start | bytes 196612
Sparse Core Ops, SparseCore 0:
  9.2 91.4 all-gather.2
  102.6 73.9 all-gather.4
where the time goes:
time: 226 us
  waiting for transfers between devices  86.8 us (38%)
  blocking collectives  33 us (15%)
  matrix products  31.3 us (14%)
  local copies, waits for them, and re-layouts  25.8 us (11%)
  starting transfers between devices  24.9 us (11%)
  between operations  16.2 us (7%)
  other arithmetic  7.65 us (3%)
    all_to_all x1, waiting for transfers between devices, from_everyone(): return lax.all_to_all(copies, axis, split_axis=0, concat_axis=0, tiled=True)  58.1 us
    all_gather x2, blocking collectives, entering(): pieces = lax.all_gather(running.astype(jnp.bfloat16), axis)  33 us
    all_gather x1, waiting for transfers between devices, per_device(): lax.all_gather(out_weight, STEP, axis=0, tiled=True)  27.1 us
    all_to_all x1, starting transfers between devices, from_everyone(): return lax.all_to_all(copies, axis, split_axis=0, concat_axis=0, tiled=True)  24.9 us
    split x3, local copies, waits for them, and re-layouts, side_by_side(): return tuple(jnp.split(gather_directly(both, axis, dim), ends, axis=along))  18.1 us
    dot_general x1, matrix products, attend_block(): jnp.einsum('hqk,khd->hqd', exp_weights.astype(jnp.bfloat16), value_split,...  11 us
    dot_general x1, matrix products, per_device(): jnp.dot(normed, lax.all_gather(query_weight, STEP, axis=0, tiled=True), p...  6.91 us
    dot_general x1, matrix products, project_back(): lax.dot_general(attended, weight_rows, (((1,), (1,)), ((), ())), preferre...  5.63 us
  transfers between devices with their start and end apart: 3, of which 2 were waited for; matrix products, arithmetic and copies ran while one was open for 24% of the time, Pallas kernels for 0%

commit v1 on v0

--- a/solution.py
+++ b/solution.py
@@ -171,7 +171,12 @@
     pieces = side_by_side((stale_keys[0], stale_values[0]), "patch", 0, 1)
     final_state = attend_block(queries, empty_state(queries), pieces[0], pieces[1])
     attended = finish_heads(final_state)
-    branch = project_back(attended, lax.all_gather(out_weight, STEP, axis=0, tiled=True))
+    branch = project_back(
+        attended,
+        jnp.concatenate(
+            lax.all_to_all(jnp.stack([out_weight] * lax.axis_size(STEP)), STEP, 0, 0), axis=0
+        ),
+    )
     mixed = hidden + gate_vec * branch
     velocity = jnp.dot(
         layer_norm(mixed).astype(jnp.bfloat16), final_weight, preferred_element_type=jnp.float32

time: 226 us -> 642 us (2.84)
  waiting for transfers between devices: 86.8 us -> 399 us
  blocking collectives: 33 us -> 134 us
    all_gather x1, waiting for transfers between devices: 0.01 us -> 274 us  [per_device(): lax.all_gather(query_weight, STEP, axis=0, tiled=True)]
    all_to_all x0 -> x1, blocking collectives: none -> 90.3 us  [from_everyone(): return lax.all_to_all(copies, axis, split_axis=0, concat_axis=0, tiled=True)]
    all_to_all x1, waiting for transfers between devices: 58.1 us -> 124 us  [per_device(): lax.all_to_all(jnp.stack([out_weight] * lax.axis_size(STEP)), STEP, 0, 0)]
    all_gather x1 -> x0, waiting for transfers between devices: 27.1 us -> none  [per_device(): lax.all_gather(out_weight, STEP, axis=0, tiled=True)]
    all_gather x2, blocking collectives: 33 us -> 43.6 us  [entering(): pieces = lax.all_gather(running.astype(jnp.bfloat16), axis)]
  transfers between devices with their start and end apart: 3 -> 2, of which waited for: 2 -> 2; matrix products, arithmetic and copies ran while one was open for 24% -> 7% of each run, Pallas kernels for 0% -> 0%
where the time goes in v1:
time: 642 us; the launch traced here: 639 us
  waiting for transfers between devices  399 us (62%)
  blocking collectives  134 us (21%)
  matrix products  31 us (5%)
  local copies, waits for them, and re-layouts  25.9 us (4%)
  starting transfers between devices  25 us (4%)
  between operations  16.4 us (3%)
  other arithmetic  7.74 us (1%)
    all_gather x1, waiting for transfers between devices, per_device(): lax.all_gather(query_weight, STEP, axis=0, tiled=True)  274 us
    all_to_all x1, waiting for transfers between devices, per_device(): lax.all_to_all(jnp.stack([out_weight] * lax.axis_size(STEP)), STEP, 0, 0)  124 us
    all_to_all x1, blocking collectives, from_everyone(): return lax.all_to_all(copies, axis, split_axis=0, concat_axis=0, tiled=True)  90.3 us
    all_gather x2, blocking collectives, entering(): pieces = lax.all_gather(running.astype(jnp.bfloat16), axis)  43.6 us
    all_to_all x1, starting transfers between devices, per_device(): lax.all_to_all(jnp.stack([out_weight] * lax.axis_size(STEP)), STEP, 0, 0)  24.9 us
    split x3, local copies, waits for them, and re-layouts, side_by_side(): return tuple(jnp.split(gather_directly(both, axis, dim), ends, axis=along))  15.8 us
  transfers between devices with their start and end apart: 2, of which 2 were waited for; matrix products, arithmetic and copies ran while one was open for 7% of the time, Pallas kernels for 0%

profile of v1, /device:TPU:36, one launch (start us, length us, event | category | flops | bytes accessed | tf_op | source)
XLA Modules:
  0.0 639.2 jit_solution(2129132933471285612)
XLA Ops:
  6.6 1.7 pad_maximum_fusion
  8.3 1.0 broadcast_in_dim.17
  9.3 90.3 %all_to_all.10 = bf16[4,320,3072]{2,1,0:T(8,128)(2,1)} all-to-all(bf16[4,320,3072]{2,1,0:T(8,128)(2,1)S(1)} %broadcast_in_dim.17), channel_id=1, replica_groups=mesh['rep'=2,'step_0'=16,'step_1'=2,'patch'=4] {'patch'}, dimensions={0} | all-to-all | bytes 15728640 | tf_op jit(solution)/shard_map/all_to_all | solution.py:18
  99.6 4.6 stack.2
  104.3 24.9 %all-to-all-start.1 = ((bf16[32,96,1536]{2,1,0:T(8,128)(2,1)}), bf16[32,96,1536]{2,1,0:T(8,128)(2,1)}, u32[]{:S(2)}, u32[]{:S(2)}) async-start(bf16[32,96,1536]{2,1,0:T(8,128)(2,1)} %stack.2), calls=%async_computation.1 | async-start | bytes 18874368 | tf_op jit(solution)/shard_map/all_to_all | solution.py:177
  129.2 0.7 all-gather.2.cloned.1.call-update
  130.6 0.7 select_reduce_fusion
  133.4 1.5 fusion.46
  135.0 0.5 multiply_reduce_fusion.2
  135.4 3.3 fusion.49
  138.7 0.9 copy-done.3
  139.6 3.6 fusion.44
  143.2 6.1 copy.31
  149.3 6.2 copy.28
  155.5 274.1 %all-gather.2.cloned.1.call-done = bf16[3072,1536]{1,0:T(8,128)(2,1)} async-done(((bf16[96,1536]{1,0:T(8,128)(2,1)}), bf16[3072,1536]{1,0:T(8,128)(2,1)}) %all-gather.2.cloned.1.call-update) | async-done | bytes 9437200 | tf_op jit(solution)/shard_map/all_gather | solution.py:167
  429.6 6.8 %fusion.7 = f32[256,1536]{0,1:T(8,128)S(1)} fusion(bf16[3072,1536]{1,0:T(8,128)(2,1)} %all-gather.2.cloned.1.call-done, f32[256,3072]{1,0:T(8,128)S(1)} %get-tuple-element.15, f32[3072]{0:T(1024)S(1)} %get-tuple-element.12, f32[3072]{0:T(1024)S(1)} %get-tuple-element.13, f32[256]{0:T(256)S(1)} %add_rsqrt_fusion.2, f32[256]{0:T(256)S(1)} %broadcast_multiply_fusion.1), kind=kOutput, calls=%fused_computation.15 | convolution fusion | flops 2419851264 | bytes 14182400 | tf_op jit(solution)/shard_map/dot_general | solution.py:165
  436.4 0.1 multiply_reduce_fusion.3
  436.6 2.4 multiply_reduce_fusion
  439.0 3.3 fusion
  442.3 2.2 copy-done.2
  444.5 10.7 %fusion.10 = bf16[256,12,128]{0,2,1:T(8,128)(2,1)} fusion(bf16[1280,12,128]{0,2,1:T(8,128)(2,1)} %bitcast.44, f32[12,256,1280]{2,1,0:T(8,128)} %copy-done.2, f32[12,256]{1,0:T(8,128)S(1)} %get-tuple-element.16, f32[256,12]{0,1:T(8,128)S(1)} %bitcast_add_fusion.1, f32[256,12]{0,1:T(8,128)S(1)} %multiply_bitcast_fusion), kind=kOutput, calls=%fused_computation.19 | convolution fusion | flops 1019609088 | bytes 20484096 | tf_op jit(solution)/shard_map/hqk,khd->hqd/dot_general | solution.py:117
  455.2 124.4 %all-to-all-done.1 = bf16[32,96,1536]{2,1,0:T(8,128)(2,1)} async-done(((bf16[32,96,1536]{2,1,0:T(8,128)(2,1)}), bf16[32,96,1536]{2,1,0:T(8,128)(2,1)}, u32[]{:S(2)}, u32[]{:S(2)}) %all-to-all-start.1) | async-done | bytes 9437216 | tf_op jit(solution)/shard_map/all_to_all | solution.py:177
  579.6 5.6 fusion.47
  585.3 0.5 multiply_reduce_fusion.1
  585.8 0.5 copy-done.5
  586.3 0.7 fusion.48
  586.9 0.1 copy.32
  587.1 0.1 convert_element_type.175
  587.2 1.9 all_gather.12
  589.1 41.7 %all_gather.13 = bf16[16,128,128]{2,1,0:T(8,128)(2,1)S(1)} all-gather(bf16[1,128,128]{2,1,0:T(8,128)(2,1)S(1)} %get-tuple-element.9), channel_id=1, replica_groups=mesh['rep'=2,'step_0'=16,'step_1'=2,'patch'=4] {'step_0'}, dimensions={0}, use_global_device_ids=true | all-gather | bytes 557056 | tf_op jit(solution)/shard_map/all_gather | solution.py:50
  631.3 0.1 fusion.36
  631.7 0.7 add_bitcast_fusion
  (42 shorter events, 1.0 us)
Async XLA Ops:
  6.5 126.9 %copy-start = (bf16[64,3072]{1,0:T(8,128)(2,1)S(1)}, bf16[64,3072]{1,0:T(8,128)(2,1)}, u32[]{:S(2)}) copy-start(bf16[64,3072]{1,0:T(8,128)(2,1)} %param.18) | copy-start | bytes 1179652
  9.3 90.3 %copy-start.6 = (bf16[96,1536]{1,0:T(8,128)(2,1)S(1)}, bf16[96,1536]{1,0:T(8,128)(2,1)}, u32[]{:S(2)}) copy-start(bf16[96,1536]{1,0:T(8,128)(2,1)} %param.24) | copy-start | bytes 884740
  104.3 26.4 %copy-start.9 = (f32[1000]{0:T(1024)S(1)}, f32[1000]{0:T(1024)}, u32[]{:S(2)}) copy-start(f32[1000]{0:T(1024)} %param.16) | copy-start | bytes 12004
  104.3 29.2 %copy-start.8 = (f32[3072]{0:T(1024)S(1)}, f32[3072]{0:T(1024)}, u32[]{:S(2)}) copy-start(f32[3072]{0:T(1024)} %param.19) | copy-start | bytes 36868
  104.3 475.4 %all-to-all-start.1 = ((bf16[32,96,1536]{2,1,0:T(8,128)(2,1)}), bf16[32,96,1536]{2,1,0:T(8,128)(2,1)}, u32[]{:S(2)}, u32[]{:S(2)}) async-start(bf16[32,96,1536]{2,1,0:T(8,128)(2,1)} %stack.2), calls=%async_computation.1 | async-start | bytes 18874368 | tf_op jit(solution)/shard_map/all_to_all | solution.py:177
  129.2 300.4 %all-gather.2.cloned.1.call-start = ((), (), s32[]{:S(2)}) async-start(), calls=%async_computation.2 | async-start | bytes 9732096 | tf_op jit(solution)/shard_map/all_gather | solution.py:167
  134.9 4.7 copy-start.3
  429.6 7.0 %copy-start.4 = (bf16[1280,1536]{0,1:T(8,128)(2,1)S(1)}, bf16[1280,1536]{0,1:T(8,128)(2,1)}, u32[]{:S(2)}) copy-start(bf16[1280,1536]{0,1:T(8,128)(2,1)} %copy.28) | copy-start | bytes 11796484
  429.6 7.0 %copy-start.10 = (f32[128]{0:T(128)S(1)}, f32[128]{0:T(128)}, u32[]{:S(2)}) copy-start(f32[128]{0:T(128)} %param.21) | copy-start | bytes 1540
  439.0 5.5 copy-start.2
  585.3 1.0 copy-start.5
  585.7 46.6 %copy-start.1 = (bf16[64,3072]{1,0:T(8,128)(2,1)S(1)}, bf16[64,3072]{1,0:T(8,128)(2,1)}, u32[]{:S(2)}) copy-start(bf16[64,3072]{1,0:T(8,128)(2,1)} %param.18) | copy-start | bytes 1179652
  586.3 45.5 %copy-start.7 = (f32[256,64]{0,1:T(8,128)S(1)}, f32[256,64]{0,1:T(8,128)}, u32[]{:S(2)}) copy-start(f32[256,64]{0,1:T(8,128)} %param.14) | copy-start | bytes 196612
Sparse Core Ops, SparseCore 0:
  131.8 297.6 all-gather.1
